TPU v7x, 32 devices: a whole 2x2x4 slice. The times are simulated.
32 devices in a mesh: grp: 4 (over z), tp: 4 (over y, x), rep: 2 (over core).
Axes of the slice: x: 2, y: 2, z: 4, core: 2. Of those that a mesh axis runs over, the one named last changes fastest.
Arguments:
- query_rows: bfloat16 [4, 1024, 2048], P('tp', ('grp', 'rep')), may hold values from -120 to 120
- key_rows: bfloat16 [4, 1024, 512], P('tp', ('grp', 'rep')), may hold values from -6 to 6, as said below
- value_rows: bfloat16 [4, 1024, 512], P('tp', ('grp', 'rep')), may hold values from -6 to 6
- teacher_codes: bfloat16 [4, 1024, 4096], P(None, ('grp', 'rep'), 'tp'), may hold values from -6 to 6
- teacher_scales: bfloat16 [4, 1024, 32], P(None, ('grp', 'rep'), 'tp'), may hold values from 0.099609375 to 1
- projection: bfloat16 [2048, 4096], P(None, ('grp', 'rep')), may hold values from -0.125 to 0.125
Outputs:
- grad_query: bfloat16 [4, 1024, 2048], P('tp', ('grp', 'rep'))
- grad_key: bfloat16 [4, 1024, 512], P('tp', ('grp', 'rep'))
- grad_value: bfloat16 [4, 1024, 512], P('tp', ('grp', 'rep'))
Inputs may be any that keep to these rules, and one draw needn't show every extreme that they name: `key_rows`: keys of every head.
All inputs are finite; a program needn't handle non-finite values.
Results may differ from a plain program's by a relative error of at most 0.014.
Values may be sent and summed in bfloat16 or wider, within the bound.
A program may use at most 128 MiB of HBM per device.

v0:
```python
import functools
import math

import jax
import jax.numpy as jnp
from jax import lax
from jax.experimental import pallas as pl
from jax.experimental.pallas import tpu as pltpu
from jax.sharding import PartitionSpec as P

HEADS = 16
KV_HEADS = 4
HEAD_DIM = 128
QBLOCK = 128


masked_low = -1e30
QUAD = 4
CHUNKS = 2


def gather_kernel(n_grp, own_ref, all_ref, local_sem, own_sems, z_send, z_recv, x_send, x_recv,
                  y_send, y_recv, d_send, d_recv, r_send, r_recv):
    g = lax.axis_index("grp")
    t = lax.axis_index("tp")
    r = lax.axis_index("rep")
    q = lax.rem(t, QUAD)
    qx = q + 1 - 2 * lax.rem(q, 2)
    qy = lax.rem(q + 2, QUAD)
    qd = lax.rem(qx + 2, QUAD)
    tx = t - q + qx
    ty = t - q + qy
    rows = own_ref.shape[0]
    size = rows // (QUAD * CHUNKS)
    others = n_grp - 1
    to_x, to_y, to_r = {"tp": tx}, {"tp": ty}, {"rep": 1 - r}
    mesh_ids = pl.DeviceIdType.MESH

    barrier = pltpu.get_barrier_semaphore()
    partners = [{"grp": lax.rem(g + k, n_grp)} for k in range(1, n_grp)] + [to_x, to_y, to_r]
    for partner in partners:
        pl.semaphore_signal(barrier, inc=1, device_id=partner, device_id_type=mesh_ids)
    pl.semaphore_wait(barrier, len(partners))

    def spot(quarter, c):
        return pl.ds(pl.multiple_of((quarter * CHUNKS + c) * size, size), size)

    def block(k):
        return lax.rem(g + k, n_grp) * 2 + r

    def sem_at(k, c):
        return c * others + k - 1

    def send(src, dst, sems, index, to):
        return pltpu.make_async_remote_copy(
            src_ref=src, dst_ref=dst, send_sem=sems[0].at[index], recv_sem=sems[1].at[index],
            device_id=to, device_id_type=mesh_ids)

    def forward(k, c, quarter, sems, index, to):
        part = all_ref.at[block(k), spot(quarter, c)]
        return send(part, part, sems, index, to)

    zs, xs, ys, ds, rs = ((z_send, z_recv), (x_send, x_recv), (y_send, y_recv),
                          (d_send, d_recv), (r_send, r_recv))
    started = []

    def go(copy):
        copy.start()
        started.append(copy)

    order = [1, n_grp - 1] + list(range(2, n_grp - 1)) if n_grp > 2 else [1]
    events = [(k, c) for c in range(CHUNKS) for k in order]
    for k, c in events:
        go(send(own_ref.at[spot(q, c)], all_ref.at[block(0), spot(q, c)], zs, sem_at(k, c),
                {"grp": lax.rem(g + n_grp - k, n_grp)}))
    local = pltpu.make_async_copy(own_ref, all_ref.at[block(0)], local_sem.at[0])
    local.start()
    own_swap = pltpu.make_async_remote_copy(
        src_ref=own_ref, dst_ref=all_ref.at[block(0)], send_sem=own_sems.at[0],
        recv_sem=own_sems.at[1], device_id=to_r, device_id_type=mesh_ids)
    own_swap.start()

    swaps = []

    def swap(k, c, quarter, lane):
        copy = forward(k, c, quarter, rs, lane * others * CHUNKS + sem_at(k, c), to_r)
        go(copy)
        swaps.append((k, c, (lane, sem_at(k, c))))

    def on_z(k, c):
        forward(k, c, q, zs, sem_at(k, c), to_x).wait_recv()
        go(forward(k, c, q, xs, sem_at(k, c), to_x))
        go(forward(k, c, q, ys, sem_at(k, c), to_y))
        swap(k, c, q, 0)

    def on_xy(k, c):
        forward(k, c, qx, xs, sem_at(k, c), to_x).wait_recv()
        if events.index((k, c)) % 2 == 0:
            go(forward(k, c, qx, ds, sem_at(k, c), to_y))
        swap(k, c, qx, 1)
        forward(k, c, qy, ys, sem_at(k, c), to_y).wait_recv()
        if events.index((k, c)) % 2 == 1:
            go(forward(k, c, qy, ds, sem_at(k, c), to_x))
        swap(k, c, qy, 2)

    def on_d(k, c):
        forward(k, c, qd, ds, sem_at(k, c), to_x).wait_recv()
        swap(k, c, qd, 3)

    lag = 2
    for i in range(len(events) + 2 * lag):
        if i < len(events):
            on_z(*events[i])
        if lag <= i < len(events) + lag:
            on_xy(*events[i - lag])
        if i >= 2 * lag:
            on_d(*events[i - 2 * lag])

    local.wait()
    own_swap.wait_send()
    for copy in started:
        copy.wait_send()
    peer = all_ref.at[lax.rem(g, n_grp) * 2 + 1 - r]
    pltpu.make_async_remote_copy(
        src_ref=own_ref, dst_ref=peer, send_sem=own_sems.at[0],
        recv_sem=own_sems.at[1], device_id=to_r, device_id_type=mesh_ids).wait_recv()
    for lane, quarter in enumerate((q, qx, qy, qd)):
        for k, c in events:
            part = all_ref.at[lax.rem(g + k, n_grp) * 2 + 1 - r, spot(quarter, c)]
            send(part, part, rs, lane * others * CHUNKS + sem_at(k, c), to_r).wait_recv()


def gather_columns(projection, n_grp, n_rep, n_tp):
    rows, width = projection.shape
    if n_rep != 2 or n_grp < 2 or n_tp % QUAD or rows % (QUAD * CHUNKS * 16):
        return lax.all_gather(projection, ("grp", "rep"), axis=0)
    steps = (n_grp - 1) * CHUNKS
    dma = pltpu.SemaphoreType.DMA
    total = n_grp * n_rep * rows * width
    return pl.pallas_call(
        functools.partial(gather_kernel, n_grp),
        out_shape=jax.ShapeDtypeStruct((n_grp * n_rep, rows, width), projection.dtype),
        in_specs=[pl.BlockSpec(memory_space=pltpu.VMEM)],
        out_specs=pl.BlockSpec(memory_space=pltpu.HBM),
        scratch_shapes=[dma((1,)), dma((2,))] + [dma((steps,))] * 8 + [dma((4 * steps,))] * 2,
        compiler_params=pltpu.CompilerParams(collective_id=0, has_side_effects=True),
        cost_estimate=pl.CostEstimate(flops=0, bytes_accessed=12 * total, transcendentals=0),
    )(projection)


def shards(mesh, query_rows, key_rows, value_rows, teacher_codes, teacher_scales, projection):
    rows_dev = query_rows.shape[1]
    group_size = HEADS // KV_HEADS
    inv_root = 1.0 / math.sqrt(HEAD_DIM)
    kv_width = key_rows.shape[2]
    pairs_all = lax.all_gather(
        jnp.concatenate([key_rows, value_rows], 2), ("grp", "rep"), axis=1, tiled=True
    )
    keys_all, values_all = pairs_all[..., :kv_width], pairs_all[..., kv_width:]
    length = keys_all.shape[1]
    my_index = lax.axis_index(("grp", "rep"))
    first_row = my_index * rows_dev
    queries = query_rows[0].reshape(rows_dev, KV_HEADS, group_size, HEAD_DIM).transpose(1, 2, 0, 3)
    key_heads = keys_all[0].reshape(length, KV_HEADS, HEAD_DIM).transpose(1, 0, 2)
    value_heads = values_all[0].reshape(length, KV_HEADS, HEAD_DIM).transpose(1, 0, 2)
    row_pos = first_row + jnp.arange(rows_dev, dtype=jnp.int32)
    slab_codes, slab_scales = (
        lax.all_to_all(teacher_codes, "tp", split_axis=0, concat_axis=2, tiled=True),
        lax.all_to_all(teacher_scales, "tp", split_axis=0, concat_axis=2, tiled=True),
    )

    raw_scores = (
        jnp.einsum("hgqd,hkd->hgqk", queries, key_heads, preferred_element_type=jnp.float32)
        * inv_root
    )
    allowed = jnp.arange(length, dtype=jnp.int32)[None, :] <= row_pos[:, None]
    scores = jnp.where(allowed, raw_scores, masked_low)
    row_peak = scores.max(-1, keepdims=True)
    shifted = jnp.exp(scores - row_peak)
    probs = shifted / shifted.sum(-1, keepdims=True)
    prob_low = probs.astype(jnp.bfloat16)
    attn_wide = jnp.einsum(
        "hgqk,hkd->hgqd", prob_low, value_heads, preferred_element_type=jnp.float32
    )
    attn_low = (
        attn_wide.transpose(2, 0, 1, 3).reshape(rows_dev, HEADS * HEAD_DIM).astype(jnp.bfloat16)
    )
    col_width = projection.shape[1]
    shaped = gather_columns(
        projection, mesh.shape["grp"], mesh.shape["rep"], mesh.shape["tp"]
    )
    pieces = shaped.shape[0]
    approx = jnp.einsum("td,sdc->tsc", attn_low, shaped, preferred_element_type=jnp.float32)
    code_rows = slab_codes[0].astype(jnp.float32)
    scale_rows = slab_scales[0].astype(jnp.float32)
    target = (code_rows.reshape(rows_dev, -1, QBLOCK) * scale_rows[..., None]).reshape(
        rows_dev, pieces, col_width
    )
    errors = (approx - target).astype(jnp.bfloat16)
    partial_terms = jnp.einsum(
        "tsc,sdc->std", errors, shaped, preferred_element_type=jnp.float32
    ).astype(jnp.bfloat16)
    grad_attn = partial_terms.astype(jnp.float32).sum(0)
    grad_low = grad_attn.astype(jnp.bfloat16)
    grad_heads = grad_low.reshape(rows_dev, KV_HEADS, group_size, HEAD_DIM).transpose(1, 2, 0, 3)
    row_delta = (grad_heads.astype(jnp.float32) * attn_wide).sum(-1)

    grad_values = jnp.einsum(
        "hgqk,hgqd->hkd", prob_low, grad_heads, preferred_element_type=jnp.float32
    )
    grad_prob = jnp.einsum(
        "hgqd,hkd->hgqk", grad_heads, value_heads, preferred_element_type=jnp.float32
    )
    grad_score = (probs * (grad_prob - row_delta[..., None]) * inv_root).astype(jnp.bfloat16)
    grad_queries = jnp.einsum(
        "hgqk,hkd->hgqd", grad_score, key_heads, preferred_element_type=jnp.float32
    )
    grad_keys = jnp.einsum(
        "hgqk,hgqd->hkd", grad_score, queries, preferred_element_type=jnp.float32
    )
    key_terms = grad_keys.transpose(1, 0, 2).reshape(1, length, KV_HEADS * HEAD_DIM)
    value_terms = grad_values.transpose(1, 0, 2).reshape(1, length, KV_HEADS * HEAD_DIM)
    pair_terms = jnp.concatenate([key_terms, value_terms], 2).astype(jnp.bfloat16)
    pair_grad = lax.psum_scatter(
        pair_terms, ("grp", "rep"), scatter_dimension=1, tiled=True
    )
    key_grad, value_grad = pair_grad[..., :kv_width], pair_grad[..., kv_width:]
    query_grad = (
        grad_queries.transpose(2, 0, 1, 3)
        .reshape(1, rows_dev, HEADS * HEAD_DIM)
        .astype(jnp.bfloat16)
    )
    return (query_grad, key_grad.astype(jnp.bfloat16), value_grad.astype(jnp.bfloat16))


def solution(mesh):
    placed = (
        P("tp", ("grp", "rep"), None),
        P("tp", ("grp", "rep"), None),
        P("tp", ("grp", "rep"), None),
        P(None, ("grp", "rep"), "tp"),
        P(None, ("grp", "rep"), "tp"),
        P(None, ("grp", "rep")),
    )
    return jax.shard_map(
        functools.partial(shards, mesh),
        mesh=mesh,
        in_specs=placed,
        out_specs=(
            P("tp", ("grp", "rep"), None),
            P("tp", ("grp", "rep"), None),
            P("tp", ("grp", "rep"), None),
        ),
        check_vma=False,
    )
```

profile of v0, /device:TPU:0, one launch (start us, length us, event | category | flops | bytes accessed | tf_op | source)
XLA Modules:
  0.0 230.5 jit_solution(67321459751837159)
XLA Ops:
  7.2 1.1 copy.42
  8.3 1.0 copy.43
  9.3 0.7 pad_maximum_fusion.1
  10.1 5.2 %all-to-all-start.1 = ((bf16[4,128,8]{1,2,0:T(8,128)(2,1)}), bf16[4,128,8]{1,2,0:T(8,128)(2,1)S(1)}, u32[]{:S(2)}, u32[]{:S(2)}) async-start(bf16[4,128,8]{1,2,0:T(8,128)(2,1)} %param.10), calls=%async_computation.1 | async-start | bytes 16384 | tf_op jit(solution)/shard_map/all_to_all | solution.py:169
  15.3 2.3 copy.49
  17.5 2.4 %all-to-all-done.1 = bf16[4,128,8]{1,2,0:T(8,128)(2,1)S(1)} async-done(((bf16[4,128,8]{1,2,0:T(8,128)(2,1)}), bf16[4,128,8]{1,2,0:T(8,128)(2,1)S(1)}, u32[]{:S(2)}, u32[]{:S(2)}) %all-to-all-start.1) | async-done | bytes 8224 | tf_op jit(solution)/shard_map/all_to_all | solution.py:169
  20.0 3.5 %all-to-all-start = ((bf16[4,128,1024]{1,2,0:T(8,128)(2,1)}), bf16[4,128,1024]{1,2,0:T(8,128)(2,1)S(1)}, u32[]{:S(2)}, u32[]{:S(2)}) async-start(bf16[4,128,1024]{1,2,0:T(8,128)(2,1)} %copy.49), calls=%async_computation | async-start | bytes 2097152 | tf_op jit(solution)/shard_map/all_to_all | solution.py:168
  23.6 1.0 copy.77
  24.6 87.2 %shard_map.85 = bf16[8,2048,512]{2,1,0:T(8,128)(2,1)} custom-call(bf16[2048,512]{1,0:T(8,128)(2,1)} %own_ref.1), custom_call_target="tpu_custom_call" | custom-call | bytes 100663296 | tf_op jit(solution)/shard_map/pallas_call | solution.py:140
  111.9 1.4 mul.36
  113.3 1.9 copy.51
  115.3 1.4 bitcast_convert_fusion.2
  116.7 2.9 %copy.50 = f32[128,8,512]{2,0,1:T(8,128)} copy(f32[128,8,512]{0,2,1:T(8,128)} %bitcast.113) | data formatting | bytes 4194304 | tf_op jit(solution)/shard_map/convert_element_type | solution.py:194
  119.6 2.7 %fusion.17 = (bf16[1,1024,512]{1,2,0:T(8,128)(2,1)}, bf16[1,1024,512]{1,2,0:T(8,128)(2,1)S(1)}) fusion(bf16[1,1024,1024]{1,2,0:T(8,128)(2,1)} %all-gather.2.cloned.1.call-done), kind=kLoop, calls=%fused_computation.28 | loop fusion | bytes 4194304 | tf_op jit(solution)/shard_map/slice | solution.py:159
  122.3 1.3 copy.44
  123.7 7.3 %fusion.19 = (f32[4,4,128]{2,1,0:T(4,128)S(1)}, f32[4,4,128,1024]{2,3,1,0:T(8,128)}) fusion(pred[128,1024]{0,1:T(8,128)(4,1)S(1)} %iota_compare_fusion, bf16[4,4,128,128]{2,3,1,0:T(8,128)(2,1)} %bitcast.121, bf16[1024,4,128]{2,0,1:T(8,128)(2,1)} %copy.44), kind=kOutput, calls=%fused_computation.30 | convolution fusion | flops 545260544 | bytes 10100736 | tf_op jit(solution)/shard_map/sub | solution.py:179
  130.9 4.5 %fusion.5 = bf16[4,4,128,1024]{2,3,1,0:T(8,128)(2,1)S(1)} fusion(f32[4,4,128,1024]{2,3,1,0:T(8,128)} %get-tuple-element.17, f32[4,4,128]{2,1,0:T(4,128)S(1)} %get-tuple-element.16), kind=kLoop, calls=%fused_computation.10 | loop fusion | flops 4194304 | bytes 12591104 | tf_op jit(solution)/shard_map/convert_element_type | solution.py:181
  135.4 1.9 copy-done
  137.4 1.9 fusion.24
  139.3 23.6 %convert_reduce_fusion = bf16[128,2048]{1,0:T(8,128)(2,1)} fusion(bf16[8,2048,512]{2,1,0:T(8,128)(2,1)} %shard_map.85, f32[128,8,512]{2,0,1:T(8,128)} %copy.50, f32[128,8,512]{2,0,1:T(8,128)S(1)} %copy.51, bf16[128,2048,1]{0,1,2:T(8,128)(2,1)} %bitcast.118), kind=kOutput, calls=%fused_computation.5 | convolution fusion | flops 4300472320 | bytes 22020096 | tf_op jit(solution)/shard_map/tsc,sdc->std/dot_general | solution.py:200
  162.9 1.3 copy.52
  164.2 1.4 multiply_reduce_fusion
  165.6 3.8 %bitcast_convert_fusion = bf16[4,1024,128]{1,2,0:T(8,128)(2,1)S(1)} fusion(bf16[4,4,128,1024]{2,3,1,0:T(8,128)(2,1)} %copy-done, bf16[4,4,128,128]{2,3,1,0:T(8,128)(2,1)S(1)} %bitcast.116), kind=kOutput, calls=%fused_computation.13 | convolution fusion | flops 537395200 | bytes 5767168 | tf_op jit(solution)/shard_map/hgqk,hgqd->hkd/dot_general | solution.py:208
  169.3 4.8 %multiply_convert_fusion = bf16[4,4,128,1024]{2,3,1,0:T(8,128)(2,1)S(1)} fusion(f32[4,4,128]{2,1,0:T(4,128)S(1)} %multiply_reduce_fusion, f32[4,4,128,1024]{2,3,1,0:T(8,128)} %get-tuple-element.17, f32[4,4,128]{2,1,0:T(4,128)S(1)} %get-tuple-element.16, bf16[4,4,128,128]{2,3,1,0:T(8,128)(2,1)S(1)} %bitcast.117, bf16[4,1024,128,1]{1,2,3,0:T(8,128)(2,1)S(1)} %bitcast.120), kind=kOutput, calls=%fused_computation.2 | convolution fusion | flops 547356672 | bytes 14172160 | tf_op jit(solution)/shard_map/hgqd,hkd->hgqk/dot_general | solution.py:211
  174.1 1.5 bitcast_convert_fusion.1
  176.1 1.3 copy.60
  177.4 0.5 copy.61
  177.9 2.9 %pad_maximum_fusion = bf16[1,1024,1024]{2,1,0:T(8,128)(2,1)} fusion(bf16[1,1024,512]{2,1,0:T(8,128)(2,1)S(1)} %copy.61, bf16[1,1024,512]{2,1,0:T(8,128)(2,1)} %copy.60), kind=kLoop, calls=%fused_computation.12 | loop fusion | flops 4194304 | bytes 4194304 | tf_op jit(solution)/shard_map/concatenate | solution.py:223
  180.8 2.9 %convolution_convert_fusion = bf16[4,4,128,128]{2,3,1,0:T(8,128)(2,1)S(1)} fusion(bf16[4,1024,128,1]{1,2,3,0:T(8,128)(2,1)S(1)} %bitcast.111, bf16[4,4,128,1024]{2,3,1,0:T(8,128)(2,1)} %copy-done.1), kind=kOutput, calls=%fused_computation.16 | convolution fusion | flops 537133056 | bytes 5767168 | tf_op jit(solution)/shard_map/hgqk,hkd->hgqd/dot_general | solution.py:215
  183.8 1.0 copy.62
  184.8 37.2 %reduce-scatter.2.cloned.1.call-done = bf16[1,128,1024]{2,1,0:T(8,128)(2,1)} async-done(((bf16[1,1024,1024]{2,1,0:T(8,128)(2,1)}), bf16[1,128,1024]{2,1,0:T(8,128)(2,1)}) %reduce-scatter.2.cloned.1.call-update) | async-done | bytes 262160 | tf_op jit(solution)/shard_map/reduce_scatter | solution.py:224
  222.0 1.7 fusion.18
  (20 shorter events, 0.7 us)
Async XLA Ops:
  7.2 16.4 %copy-start.5 = (bf16[1,128,2048]{2,1,0:T(8,128)(2,1)S(1)}, bf16[1,128,2048]{2,1,0:T(8,128)(2,1)}, u32[]{:S(2)}) copy-start(bf16[1,128,2048]{2,1,0:T(8,128)(2,1)} %param.6) | copy-start | bytes 1572868
  7.2 112.4 %all-gather.2.cloned.1.call-start = ((), (), s32[]{:S(2)}) async-start(), calls=%async_computation.3 | async-start | bytes 2359296 | tf_op jit(solution)/shard_map/all_gather | solution.py:156
  10.1 9.9 %all-to-all-start.1 = ((bf16[4,128,8]{1,2,0:T(8,128)(2,1)}), bf16[4,128,8]{1,2,0:T(8,128)(2,1)S(1)}, u32[]{:S(2)}, u32[]{:S(2)}) async-start(bf16[4,128,8]{1,2,0:T(8,128)(2,1)} %param.10), calls=%async_computation.1 | async-start | bytes 16384 | tf_op jit(solution)/shard_map/all_to_all | solution.py:169
  20.0 95.3 %all-to-all-start = ((bf16[4,128,1024]{1,2,0:T(8,128)(2,1)}), bf16[4,128,1024]{1,2,0:T(8,128)(2,1)S(1)}, u32[]{:S(2)}, u32[]{:S(2)}) async-start(bf16[4,128,1024]{1,2,0:T(8,128)(2,1)} %copy.49), calls=%async_computation | async-start | bytes 2097152 | tf_op jit(solution)/shard_map/all_to_all | solution.py:168
  23.5 198.5 %reduce-scatter.2.cloned.1.call-start = ((), (), s32[]{:S(2)}) async-start(), calls=%async_computation.4 | async-start | bytes 2359296 | tf_op jit(solution)/shard_map/reduce_scatter | solution.py:224
  130.9 6.5 %copy-start.2 = (bf16[1,1024,512]{1,2,0:T(8,128)(2,1)S(1)}, bf16[1,1024,512]{1,2,0:T(8,128)(2,1)}, u32[]{:S(2)}) copy-start(bf16[1,1024,512]{1,2,0:T(8,128)(2,1)} %get-tuple-element.12) | copy-start | bytes 3145732
  135.4 2.0 copy-start
  165.5 3.8 %copy-start.3 = (bf16[1,1024,512]{1,2,0:T(8,128)(2,1)S(1)}, bf16[1,1024,512]{1,2,0:T(8,128)(2,1)}, u32[]{:S(2)}) copy-start(bf16[1,1024,512]{1,2,0:T(8,128)(2,1)} %get-tuple-element.12) | copy-start | bytes 3145732
  169.3 4.8 %copy-start.4 = (bf16[1,128,2048]{1,2,0:T(8,128)(2,1)S(1)}, bf16[1,128,2048]{1,2,0:T(8,128)(2,1)}, u32[]{:S(2)}) copy-start(bf16[1,128,2048]{1,2,0:T(8,128)(2,1)} %copy.77) | copy-start | bytes 1572868
  174.1 1.9 copy-start.1
Sparse Core Ops, SparseCore 0:
  10.2 52.3 all-gather.1
  180.9 41.0 reduce-scatter.1
where the time goes:
time: 231 us
  Pallas kernels  87.2 us (38%)
  matrix products  45.7 us (20%)
  waiting for transfers between devices  39.7 us (17%)
  local copies, waits for them, and re-layouts  23.9 us (10%)
  between operations  14.2 us (6%)
  other arithmetic  11 us (5%)
  starting transfers between devices  8.8 us (4%)
    pallas_call x1, Pallas kernels, gather_columns(): pl.pallas_call(functools.partial(gather_kernel, n_grp), out_shape=jax.Sha...  87.2 us
    reduce_scatter x1, waiting for transfers between devices, shards(): lax.psum_scatter(pair_terms, ('grp', 'rep'), scatter_dimension=1, tiled=T...  37.2 us
    dot_general x1, matrix products, shards(): jnp.einsum('tsc,sdc->std', errors, shaped, preferred_element_type=jnp.flo...  23.6 us
    unnamed x16, local copies, waits for them, and re-layouts  7.78 us
    sub x1, matrix products, shards(): shifted = jnp.exp(scores - row_peak)  7.26 us
    all_to_all x1, starting transfers between devices, shards(): lax.all_to_all(teacher_scales, 'tp', split_axis=0, concat_axis=2, tiled=T...  5.2 us
    dot_general x1, matrix products, shards(): jnp.einsum('hgqd,hkd->hgqk', grad_heads, value_heads, preferred_element_t...  4.78 us
  transfers between devices with their start and end apart: 4, of which 2 were waited for; matrix products, arithmetic and copies ran while one was open for 7% of the time, Pallas kernels for 38%

commit v1 on v0

--- a/solution.py
+++ b/solution.py
@@ -148,7 +148,402 @@
     )(projection)
 
 
+NEAR = 4
+SUBS = 4
+
+
+def fused_kernel(n_grp, n_tp, q_in, k_in, v_in, codes_in, scales_ref, proj_in, dq_ref, dk_ref, dv_ref,
+                 q_v, k_all, v_all, codes_v, stage, pq, probs, wide, gathered, acc, errs, terms, sums,
+                 pieces, peer_pieces, above, below, lsem, kvz_s, kvz_r, kvd_s, kvd_r, up_s, down_s, z_r,
+                 px_s, px_r, pd_s, pd_r, lp_s, ag_s, ag_r, rs_s, rs_r, gd_s, gd_r, gz_s, gz_r):
+    g = lax.axis_index("grp")
+    t = lax.axis_index("tp")
+    r = lax.axis_index("rep")
+    rows = q_v.shape[0]
+    head_dim = HEAD_DIM
+    per = HEADS // KV_HEADS
+    feats = per * head_dim
+    slabs = codes_v.shape[0]
+    width = codes_v.shape[2]
+    half = proj_in.shape[1]
+    piece = proj_in.shape[0] // n_tp
+    sub = piece // SUBS
+    length = k_all.shape[0]
+    inv_root = 1.0 / math.sqrt(head_dim)
+    mesh_ids = pl.DeviceIdType.MESH
+    other = {"rep": 1 - r}
+    up = {"grp": jnp.minimum(g + 1, n_grp - 1)}
+    down = {"grp": jnp.maximum(g - 1, 0)}
+    has_up = g < n_grp - 1
+    has_down = g > 0
+
+    def peer_tp(m):
+        return {"tp": lax.rem(t + m, n_tp)}
+
+    def sender(m):
+        return lax.rem(t + n_tp - m, n_tp)
+
+    def send(src, dst, send_sem, recv_sem, to):
+        return pltpu.make_async_remote_copy(src_ref=src, dst_ref=dst, send_sem=send_sem, recv_sem=recv_sem,
+                                            device_id=to, device_id_type=mesh_ids)
+
+    def arrived(dst, send_sem, recv_sem):
+        send(dst, dst, send_sem, recv_sem, other).wait_recv()
+
+    ended = []
+
+    def go(copy, when=None):
+        if when is None:
+            copy.start()
+        else:
+            pl.when(when)(copy.start)
+        ended.append((copy, when))
+
+    def block(s, core):
+        return pl.ds(pl.multiple_of((s * 2 + core) * rows, rows), rows)
+
+    def local(src, dst, index):
+        copy = pltpu.make_async_copy(src, dst, lsem.at[index])
+        copy.start()
+        return copy
+
+    own_k = local(k_in.at[0], k_all.at[block(g, r)], 0)
+    own_v = local(v_in.at[0], v_all.at[block(g, r)], 1)
+    own_q = local(q_in.at[0], q_v, 2)
+    own_codes = local(codes_in, codes_v, 3)
+    own_cols = pltpu.make_async_copy(proj_in, pq.at[r], lsem.at[4])
+    mine = t == g
+    pl.when(mine)(own_cols.start)
+
+    barrier = pltpu.get_barrier_semaphore()
+    for to, when in [(other, None), (up, has_up), (down, has_down)] + [(peer_tp(m), None) for m in range(1, n_tp)]:
+        def greet(to=to):
+            pl.semaphore_signal(barrier, inc=1, device_id=to, device_id_type=mesh_ids)
+        if when is None:
+            greet()
+        else:
+            pl.when(when)(greet)
+    pl.semaphore_wait(barrier, n_tp + has_up.astype(jnp.int32) + has_down.astype(jnp.int32))
+
+    kv = ((k_in, k_all), (v_in, v_all))
+    for i, (src, dst) in enumerate(kv):
+        go(send(src.at[0], dst.at[block(g, r)], kvz_s.at[i, g], kvz_r.at[i, g], up), has_up)
+    for i, (src, dst) in enumerate(kv):
+        go(send(src.at[0], dst.at[block(g, r)], kvd_s.at[i, g], kvd_r.at[i, g], other))
+
+    def own_piece(k):
+        return proj_in.at[pl.ds(pl.multiple_of(t * piece + k * sub, sub), sub)]
+
+    def held(s, k):
+        return stage.at[s, pl.ds(k * sub, sub)]
+
+    def placed(core, c, k):
+        return pq.at[core, pl.ds(pl.multiple_of(c * piece + k * sub, sub), sub)]
+
+    for k in range(SUBS):
+        go(send(own_piece(k), held(g, k), down_s.at[g, k], z_r.at[g, k], down), has_down)
+    for c in range(n_tp):
+        for k in range(SUBS):
+            rows_ck = pl.ds(c * piece + k * sub, sub)
+            go(send(proj_in.at[rows_ck], placed(r, c, k), pd_s.at[c, k], pd_r.at[c, k], other), mine)
+
+    for s in range(1, n_grp):
+        @pl.when(s > g)
+        def _():
+            span = pl.ds(s * 2 * rows, 2 * rows)
+            k_all[span] = jnp.zeros((2 * rows, k_all.shape[1]), k_all.dtype)
+            v_all[span] = jnp.zeros((2 * rows, v_all.shape[1]), v_all.dtype)
+
+    own_codes.wait()
+    for b in range(width // QBLOCK):
+        at = pl.ds(b * QBLOCK, QBLOCK)
+        for u in range(slabs):
+            acc[u * rows:(u + 1) * rows, at] = -(codes_v[u, :, at].astype(jnp.float32)
+                                                * scales_ref[u, :, b:b + 1].astype(jnp.float32))
+
+    for d in range(1, n_grp):
+        s = jnp.maximum(g - d, 0)
+        here = g >= d
+        for i, (_, dst) in enumerate(kv):
+            part = dst.at[block(s, r)]
+            pl.when(here)(functools.partial(arrived, part, kvz_s.at[i, s], kvz_r.at[i, s]))
+            go(send(part, part, kvz_s.at[i, s], kvz_r.at[i, s], up), jnp.logical_and(here, has_up))
+            go(send(part, part, kvd_s.at[i, s], kvd_r.at[i, s], other), here)
+
+    def own_up(k):
+        go(send(own_piece(k), held(g, k), up_s.at[g, k], z_r.at[g, k], up), has_up)
+
+    for k in range(SUBS // 2):
+        own_up(k)
+
+    own_k.wait()
+    own_v.wait()
+    own_q.wait()
+    for s in range(n_grp):
+        for i, (_, dst) in enumerate(kv):
+            part = dst.at[block(s, 1 - r)]
+            pl.when(s <= g)(functools.partial(arrived, part, kvd_s.at[i, s], kvd_r.at[i, s]))
+
+    first = (g * 2 + r) * rows
+    row_pos = first + lax.rem(lax.broadcasted_iota(jnp.int32, (per * rows, length), 0), rows)
+    allowed = lax.broadcasted_iota(jnp.int32, (per * rows, length), 1) <= row_pos
+
+    def head_cols(kh, j=0):
+        return pl.ds(pl.multiple_of(kh * feats + j * head_dim, head_dim), head_dim)
+
+    def kv_cols(kh):
+        return pl.ds(pl.multiple_of(kh * head_dim, head_dim), head_dim)
+
+    def stacked_queries(kh):
+        return jnp.concatenate([q_v[:, head_cols(kh, j)] for j in range(per)], axis=0)
+
+    def ag_copy(kh, m):
+        part = gathered.at[t, kh]
+        return send(part, part, ag_s.at[m - 1, kh], ag_r.at[m - 1, kh], peer_tp(m))
+
+    def forward(kh, carry):
+        scores = lax.dot_general(stacked_queries(kh), k_all[:, kv_cols(kh)], (((1,), (1,)), ((), ())),
+                                 preferred_element_type=jnp.float32) * inv_root
+        scores = jnp.where(allowed, scores, masked_low)
+        shifted = jnp.exp(scores - scores.max(-1, keepdims=True))
+        low = (shifted / shifted.sum(-1, keepdims=True)).astype(jnp.bfloat16)
+        probs[kh] = low
+        out = jnp.dot(low, v_all[:, kv_cols(kh)], preferred_element_type=jnp.float32)
+        wide[kh] = out
+        out_low = out.astype(jnp.bfloat16)
+        for j in range(per):
+            gathered[t, kh, :, j * head_dim:(j + 1) * head_dim] = out_low[j * rows:(j + 1) * rows]
+        for m in range(1, n_tp):
+            ag_copy(kh, m).start()
+        return carry
+
+    lax.fori_loop(0, KV_HEADS, forward, 0)
+
+    def pass_on(c, k):
+        part = placed(r, c, k)
+        arrived(part, px_s.at[0, k], px_r.at[c, k])
+        send(part, part, pd_s.at[c, k], pd_r.at[c, k], other).start()
+
+    def others(k):
+        for m in range(1, n_tp):
+            pass_on(sender(m), k)
+
+    def event(s, here, k, onward, onward_sem, to):
+        part = held(s, k)
+        pl.when(here)(functools.partial(arrived, part, up_s.at[s, k], z_r.at[s, k]))
+        go(send(part, part, onward_sem.at[s, k], z_r.at[s, k], to), jnp.logical_and(here, onward))
+        keep = jnp.logical_and(here, s == t)
+        give = jnp.logical_and(here, s != t)
+        go(send(part, placed(r, t, k), px_s.at[s, k], px_r.at[t, k], {"tp": s}), give)
+
+        @pl.when(keep)
+        def _():
+            pltpu.make_async_copy(part, placed(r, t, k), lp_s.at[k]).start()
+            send(part, placed(r, t, k), pd_s.at[t, k], pd_r.at[t, k], other).start()
+            if k > 0:
+                others(k - 1)
+
+    def from_above(d, k):
+        event(jnp.minimum(g + d, n_grp - 1), g + d < n_grp, k, has_down, down_s, down)
+
+    def from_below(d, k):
+        event(jnp.maximum(g - d, 0), g >= d, k, has_up, up_s, up)
+
+    for k in range(SUBS):
+        from_above(1, k)
+    for k in range(SUBS // 2, SUBS):
+        own_up(k)
+    for k in range(SUBS):
+        for d in range(1, n_grp):
+            from_below(d, k)
+    for d in range(2, n_grp):
+        for k in range(SUBS):
+            from_above(d, k)
+
+    foreign = t != g
+
+    @pl.when(foreign)
+    def _():
+        others(SUBS - 1)
+        for k in range(SUBS):
+            pltpu.make_async_copy(held(t, k), placed(r, t, k), lp_s.at[k]).wait()
+
+    pl.when(mine)(own_cols.wait)
+    for c in range(n_tp):
+        for k in range(SUBS):
+            arrived(placed(1 - r, c, k), pd_s.at[c, k], pd_r.at[c, k])
+
+    def proj_rows(kh):
+        return pl.ds(pl.multiple_of(kh * feats, feats), feats)
+
+    def project(kh, carry):
+        for m in range(1, n_tp):
+            arrived(gathered.at[sender(m), kh], ag_s.at[m - 1, kh], ag_r.at[m - 1, kh])
+        left = jnp.concatenate([gathered[u, kh] for u in range(slabs)], axis=0)
+        for b in range(2):
+            acc[:, b * half:(b + 1) * half] += jnp.dot(left, pq[b, proj_rows(kh)],
+                                                       preferred_element_type=jnp.float32)
+        return carry
+
+    lax.fori_loop(0, KV_HEADS, project, 0)
+    errs[...] = acc[...].astype(jnp.bfloat16)
+
+    def rs_copy(kh, m):
+        return send(terms.at[kh, lax.rem(t + m, n_tp)], sums.at[kh, m - 1], rs_s.at[m - 1, kh],
+                    rs_r.at[m - 1, kh], peer_tp(m))
+
+    def back_project(kh, carry):
+        total = jnp.zeros((slabs * rows, feats), jnp.float32)
+        for b in range(2):
+            total += lax.dot_general(errs[:, b * half:(b + 1) * half], pq[b, proj_rows(kh)],
+                                     (((1,), (1,)), ((), ())), preferred_element_type=jnp.float32)
+        for u in range(slabs):
+            terms[kh, u] = total[u * rows:(u + 1) * rows].astype(jnp.bfloat16)
+        for m in range(1, n_tp):
+            rs_copy(kh, m).start()
+        return carry
+
+    lax.fori_loop(0, KV_HEADS, back_project, 0)
+
+    def gd_copy(kh):
+        return send(pieces.at[kh, 1 - r], peer_pieces.at[kh], gd_s.at[kh], gd_r.at[kh], other)
+
+    def backward(kh):
+        grad = terms[kh, t].astype(jnp.float32)
+        for m in range(1, n_tp):
+            arrived(sums.at[kh, m - 1], rs_s.at[m - 1, kh], rs_r.at[m - 1, kh])
+            grad += sums[kh, m - 1].astype(jnp.float32)
+        grad = grad.astype(jnp.bfloat16)
+        grad = jnp.concatenate([grad[:, j * head_dim:(j + 1) * head_dim] for j in range(per)], axis=0)
+        delta = (grad.astype(jnp.float32) * wide[kh]).sum(-1, keepdims=True)
+        low = probs[kh]
+        grad_prob = lax.dot_general(grad, v_all[:, kv_cols(kh)], (((1,), (1,)), ((), ())),
+                                    preferred_element_type=jnp.float32)
+        score = (low.astype(jnp.float32) * (grad_prob - delta) * inv_root).astype(jnp.bfloat16)
+        dq = jnp.dot(score, k_all[:, kv_cols(kh)], preferred_element_type=jnp.float32).astype(jnp.bfloat16)
+        for j in range(per):
+            dq_ref[0, :, head_cols(kh, j)] = dq[j * rows:(j + 1) * rows]
+        over_rows = (((0,), (0,)), ((), ()))
+        for i, (lhs, rhs) in enumerate(((stacked_queries(kh), score), (grad, low))):
+            term = lax.dot_general(lhs, rhs, over_rows, preferred_element_type=jnp.float32).astype(jnp.bfloat16)
+            for s in range(n_grp):
+                for core in range(2):
+                    at = (s * 2 + core) * rows
+                    pieces[kh, core, s, i * head_dim:(i + 1) * head_dim, :] = term[:, at:at + rows]
+        gd_copy(kh).start()
+
+    def gz_copy(kh, s):
+        return send(below.at[kh, s], above.at[kh, s], gz_s.at[kh, s], gz_r.at[kh, s], down)
+
+    def reduce(kh):
+        arrived(peer_pieces.at[kh], gd_s.at[kh], gd_r.at[kh])
+        for s in range(n_grp):
+            @pl.when(s <= g)
+            def _():
+                total = pieces[kh, r, s].astype(jnp.float32) + peer_pieces[kh, s].astype(jnp.float32)
+                wide_sum[...] = total
+
+                @pl.when(has_up)
+                def _():
+                    arrived(above.at[kh, s], gz_s.at[kh, s], gz_r.at[kh, s])
+                    wide_sum[...] += above[kh, s].astype(jnp.float32)
+
+                @pl.when(s < g)
+                def _():
+                    below[kh, s] = wide_sum[...].astype(jnp.bfloat16)
+                    gz_copy(kh, s).start()
+
+                @pl.when(s == g)
+                def _():
+                    done = wide_sum[...]
+                    dk_ref[0, :, kv_cols(kh)] = done[:head_dim].T.astype(jnp.bfloat16)
+                    dv_ref[0, :, kv_cols(kh)] = done[head_dim:].T.astype(jnp.bfloat16)
+
+    def last(kh, carry):
+        pl.when(kh < KV_HEADS)(lambda: backward(kh))
+        pl.when(kh > 0)(lambda: reduce(kh - 1))
+        return carry
+
+    wide_sum = acc.at[pl.ds(0, 2 * head_dim), pl.ds(0, rows)]
+    lax.fori_loop(0, KV_HEADS + 1, last, 0)
+
+    for copy, when in ended:
+        if when is None:
+            copy.wait_send()
+        else:
+            pl.when(when)(copy.wait_send)
+
+    @pl.when(foreign)
+    def _():
+        for c in range(n_tp):
+            for k in range(SUBS):
+                part = placed(r, c, k)
+                send(part, part, pd_s.at[c, k], pd_r.at[c, k], other).wait_send()
+
+    def sent(kh, carry):
+        for m in range(1, n_tp):
+            ag_copy(kh, m).wait_send()
+            rs_copy(kh, m).wait_send()
+        gd_copy(kh).wait_send()
+        for s in range(n_grp):
+            pl.when(s < g)(lambda s=s: gz_copy(kh, s).wait_send())
+        return carry
+
+    lax.fori_loop(0, KV_HEADS, sent, 0)
+
+
+def fused(mesh, query_rows, key_rows, value_rows, teacher_codes, teacher_scales, projection):
+    n_grp, n_tp = mesh.shape["grp"], mesh.shape["tp"]
+    rows, depth = query_rows.shape[1:]
+    kv_width = key_rows.shape[2]
+    slabs, _, width = teacher_codes.shape
+    half = projection.shape[1]
+    length = n_grp * 2 * rows
+    per = HEADS // KV_HEADS
+    feats = per * HEAD_DIM
+    piece = depth // n_tp
+    low, wide = jnp.bfloat16, jnp.float32
+    vmem = pltpu.VMEM
+    dma = pltpu.SemaphoreType.DMA
+    hbm_spec = pl.BlockSpec(memory_space=pl.ANY)
+    vmem_spec = pl.BlockSpec(memory_space=pltpu.VMEM)
+    scratch = [
+        vmem((rows, depth), low), vmem((length, kv_width), low), vmem((length, kv_width), low),
+        vmem((slabs, rows, width), low), vmem((n_grp, piece, half), low), vmem((2, depth, half), low),
+        vmem((KV_HEADS, per * rows, length), low), vmem((KV_HEADS, per * rows, HEAD_DIM), wide),
+        vmem((slabs, KV_HEADS, rows, feats), low), vmem((slabs * rows, width), wide),
+        vmem((slabs * rows, width), low), vmem((KV_HEADS, slabs, rows, feats), low),
+        vmem((KV_HEADS, n_tp - 1, rows, feats), low), vmem((KV_HEADS, 2, n_grp, 2 * HEAD_DIM, rows), low),
+        vmem((KV_HEADS, n_grp, 2 * HEAD_DIM, rows), low), vmem((KV_HEADS, n_grp, 2 * HEAD_DIM, rows), low),
+        vmem((KV_HEADS, n_grp, 2 * HEAD_DIM, rows), low),
+        dma((5,)), dma((2, n_grp)), dma((2, n_grp)), dma((2, n_grp)), dma((2, n_grp)),
+        dma((n_grp, SUBS)), dma((n_grp, SUBS)), dma((n_grp, SUBS)),
+        dma((n_grp, SUBS)), dma((n_tp, SUBS)), dma((n_tp, SUBS)), dma((n_tp, SUBS)), dma((SUBS,)),
+        dma((n_tp - 1, KV_HEADS)), dma((n_tp - 1, KV_HEADS)), dma((n_tp - 1, KV_HEADS)),
+        dma((n_tp - 1, KV_HEADS)), dma((KV_HEADS,)), dma((KV_HEADS,)),
+        dma((KV_HEADS, n_grp)), dma((KV_HEADS, n_grp)),
+    ]
+    return pl.pallas_call(
+        functools.partial(fused_kernel, n_grp, n_tp),
+        out_shape=[jax.ShapeDtypeStruct(a.shape, a.dtype) for a in (query_rows, key_rows, value_rows)],
+        in_specs=[hbm_spec] * 4 + [vmem_spec, hbm_spec],
+        out_specs=[vmem_spec] * 3,
+        scratch_shapes=scratch,
+        compiler_params=pltpu.CompilerParams(collective_id=1, has_side_effects=True,
+                                             vmem_limit_bytes=60 * 2 ** 20),
+    )(query_rows, key_rows, value_rows, teacher_codes, teacher_scales, projection)
+
+
+def suits(mesh, teacher_codes, projection):
+    depth, half = projection.shape
+    n_grp, n_tp, n_rep = (mesh.shape[axis] for axis in ("grp", "tp", "rep"))
+    return (n_rep == 2 and 1 < n_grp == n_tp <= NEAR and teacher_codes.shape[2] == 2 * half
+            and depth % (n_tp * SUBS * 16) == 0)
+
+
 def shards(mesh, query_rows, key_rows, value_rows, teacher_codes, teacher_scales, projection):
+    if suits(mesh, teacher_codes, projection):
+        return tuple(fused(mesh, query_rows, key_rows, value_rows, teacher_codes, teacher_scales, projection))
     rows_dev = query_rows.shape[1]
     group_size = HEADS // KV_HEADS
     inv_root = 1.0 / math.sqrt(HEAD_DIM)

time: 231 us -> 156 us (0.68)
  Pallas kernels: 87.2 us -> 149 us
  matrix products: 45.7 us -> 0 us
  waiting for transfers between devices: 39.7 us -> 0 us
  local copies, waits for them, and re-layouts: 23.9 us -> 6.51 us
  between operations: 14.2 us -> 0.64 us
  other arithmetic: 11 us -> 0 us
  starting transfers between devices: 8.8 us -> 0 us
    pallas_call x1, Pallas kernels: 87.2 us -> 149 us  [fused(): pl.pallas_call(functools.partial(fused_kernel, n_grp, n_tp), out_shape=[j...]
    dot_general x6 -> x0, matrix products: 38.5 us -> none  [the longest x1 23.6 us: shards(): jnp.einsum('tsc,sdc->std', errors, shaped, preferred_element_type=jnp.flo...]
    reduce_scatter x1 -> x0, waiting for transfers between devices: 37.2 us -> none  [shards(): lax.psum_scatter(pair_terms, ('grp', 'rep'), scatter_dimension=1, tiled=T...]
    all_to_all x2 -> x0, starting transfers between devices: 8.72 us -> none  [the longest x1 5.2 us: shards(): lax.all_to_all(teacher_scales, 'tp', split_axis=0, concat_axis=2, tiled=T...]
    sub x1 -> x0, matrix products: 7.26 us -> none  [shards(): shifted = jnp.exp(scores - row_peak)]
    convert_element_type x3 -> x0, other arithmetic: 5.92 us -> none  [the longest x1 4.48 us: shards(): prob_low = probs.astype(jnp.bfloat16)]
    slice x2 -> x0, local copies, waits for them, and re-layouts: 4.39 us -> none  [the longest x1 2.71 us: shards(): pairs_all[..., kv_width:]]
    concatenate x2 -> x0, other arithmetic: 3.58 us -> none  [the longest x1 2.87 us: shards(): jnp.concatenate([key_terms, value_terms], 2).astype(jnp.bfloat16)]
  transfers between devices with their start and end apart: 4 -> 0, of which waited for: 2 -> 0; matrix products, arithmetic and copies ran while one was open for 7% -> 0% of each run, Pallas kernels for 38% -> 0%
where the time goes in v1:
time: 156 us
  Pallas kernels  149 us (96%)
  local copies, waits for them, and re-layouts  6.51 us (4%)
    pallas_call x1, Pallas kernels, fused(): pl.pallas_call(functools.partial(fused_kernel, n_grp, n_tp), out_shape=[j...  149 us
    unnamed x4, local copies, waits for them, and re-layouts  6.51 us

profile of v1, /device:TPU:0, one launch (start us, length us, event | category | flops | bytes accessed | tf_op | source)
XLA Modules:
  0.0 155.8 jit_solution(9049107605363556332)
XLA Ops:
  0.6 1.5 copy.9.scales_ref
  2.1 148.6 %shard_map.85 = (bf16[1,128,2048]{2,1,0:T(8,128)(2,1)}, bf16[1,128,512]{2,1,0:T(8,128)(2,1)}, bf16[1,128,512]{2,1,0:T(8,128)(2,1)}) custom-call(bf16[1,128,2048]{2,1,0:T(8,128)(2,1)} %q_in.1, bf16[1,128,512]{2,1,0:T(8,128)(2,1)} %k_in.1, bf16[1,128,512]{2,1,0:T(8,128)(2,1)} %v_in.1, bf16[4,128,1024]{2,1,0:T(8,128)(2,1)} %codes_in.1, ...), custom_call_target="tpu_custom_call" | custom-call | tf_op jit(solution)/shard_map/pallas_call | solution.py:526
  150.7 1.9 %copy.13 = bf16[1,128,2048]{2,1,0:T(8,128)(2,1)} copy(bf16[1,128,2048]{2,1,0:T(8,128)(2,1)} %get-tuple-element.6) | data formatting | bytes 1048576
  152.6 1.6 %copy.14 = bf16[1,128,512]{2,1,0:T(8,128)(2,1)} copy(bf16[1,128,512]{2,1,0:T(8,128)(2,1)} %get-tuple-element.7) | data formatting | bytes 262144
  154.2 1.6 %copy.15 = bf16[1,128,512]{2,1,0:T(8,128)(2,1)} copy(bf16[1,128,512]{2,1,0:T(8,128)(2,1)} %get-tuple-element.8) | data formatting | bytes 262144

commit v2 on v1

--- a/solution.py
+++ b/solution.py
@@ -152,10 +152,10 @@
 SUBS = 4
 
 
-def fused_kernel(n_grp, n_tp, q_in, k_in, v_in, codes_in, scales_ref, proj_in, dq_ref, dk_ref, dv_ref,
-                 q_v, k_all, v_all, codes_v, stage, pq, probs, wide, gathered, acc, errs, terms, sums,
+def fused_kernel(n_grp, n_tp, q_in, k_in, v_in, codes_in, scales_in, proj_in, dq_ref, dk_ref, dv_ref,
+                 q_v, k_all, v_all, codes_v, scales_ref, pq, probs, wide, gathered, acc, errs, terms, sums,
                  pieces, peer_pieces, above, below, lsem, kvz_s, kvz_r, kvd_s, kvd_r, up_s, down_s, z_r,
-                 px_s, px_r, pd_s, pd_r, lp_s, ag_s, ag_r, rs_s, rs_r, gd_s, gd_r, gz_s, gz_r):
+                 pd_s, pd_r, ag_s, ag_r, rs_s, rs_r, gd_s, gd_r, gz_s, gz_r):
     g = lax.axis_index("grp")
     t = lax.axis_index("tp")
     r = lax.axis_index("rep")
@@ -166,8 +166,8 @@
     slabs = codes_v.shape[0]
     width = codes_v.shape[2]
     half = proj_in.shape[1]
-    piece = proj_in.shape[0] // n_tp
-    sub = piece // SUBS
+    steps = KV_HEADS * SUBS
+    sub = proj_in.shape[0] // steps
     length = k_all.shape[0]
     inv_root = 1.0 / math.sqrt(head_dim)
     mesh_ids = pl.DeviceIdType.MESH
@@ -211,19 +211,16 @@
     own_v = local(v_in.at[0], v_all.at[block(g, r)], 1)
     own_q = local(q_in.at[0], q_v, 2)
     own_codes = local(codes_in, codes_v, 3)
-    own_cols = pltpu.make_async_copy(proj_in, pq.at[r], lsem.at[4])
+    own_scales = local(scales_in, scales_ref, 4)
+    own_cols = pltpu.make_async_copy(proj_in, pq.at[r], lsem.at[5])
     mine = t == g
     pl.when(mine)(own_cols.start)
 
     barrier = pltpu.get_barrier_semaphore()
-    for to, when in [(other, None), (up, has_up), (down, has_down)] + [(peer_tp(m), None) for m in range(1, n_tp)]:
-        def greet(to=to):
-            pl.semaphore_signal(barrier, inc=1, device_id=to, device_id_type=mesh_ids)
-        if when is None:
-            greet()
-        else:
-            pl.when(when)(greet)
-    pl.semaphore_wait(barrier, n_tp + has_up.astype(jnp.int32) + has_down.astype(jnp.int32))
+    greeted = [other] + [peer_tp(m) for m in range(1, n_tp)] + [{"grp": lax.rem(g + m, n_grp)} for m in range(1, n_grp)]
+    for to in greeted:
+        pl.semaphore_signal(barrier, inc=1, device_id=to, device_id_type=mesh_ids)
+    pl.semaphore_wait(barrier, len(greeted))
 
     kv = ((k_in, k_all), (v_in, v_all))
     for i, (src, dst) in enumerate(kv):
@@ -231,35 +228,40 @@
     for i, (src, dst) in enumerate(kv):
         go(send(src.at[0], dst.at[block(g, r)], kvd_s.at[i, g], kvd_r.at[i, g], other))
 
-    def own_piece(k):
-        return proj_in.at[pl.ds(pl.multiple_of(t * piece + k * sub, sub), sub)]
-
-    def held(s, k):
-        return stage.at[s, pl.ds(k * sub, sub)]
-
-    def placed(core, c, k):
-        return pq.at[core, pl.ds(pl.multiple_of(c * piece + k * sub, sub), sub)]
-
-    for k in range(SUBS):
-        go(send(own_piece(k), held(g, k), down_s.at[g, k], z_r.at[g, k], down), has_down)
-    for c in range(n_tp):
-        for k in range(SUBS):
-            rows_ck = pl.ds(c * piece + k * sub, sub)
-            go(send(proj_in.at[rows_ck], placed(r, c, k), pd_s.at[c, k], pd_r.at[c, k], other), mine)
+    def span(k):
+        return pl.ds(k * sub if isinstance(k, int) else pl.multiple_of(k * sub, sub), sub)
+
+    def placed(core, k):
+        return pq.at[core, span(k)]
+
+    def own_down(k):
+        return send(proj_in.at[span(k)], placed(r, k), down_s.at[k], z_r.at[k], down)
+
+    def own_up(k):
+        return send(proj_in.at[span(k)], placed(r, k), up_s.at[k], z_r.at[k], up)
+
+    def own_over(k):
+        return send(proj_in.at[span(k)], placed(r, k), pd_s.at[k], pd_r.at[k], other)
+
+    for k in range(steps):
+        go(own_down(k), jnp.logical_and(mine, has_down))
+    for k in range(steps):
+        go(own_over(k), mine)
 
     for s in range(1, n_grp):
         @pl.when(s > g)
         def _():
-            span = pl.ds(s * 2 * rows, 2 * rows)
-            k_all[span] = jnp.zeros((2 * rows, k_all.shape[1]), k_all.dtype)
-            v_all[span] = jnp.zeros((2 * rows, v_all.shape[1]), v_all.dtype)
+            unseen = pl.ds(s * 2 * rows, 2 * rows)
+            k_all[unseen] = jnp.zeros((2 * rows, k_all.shape[1]), k_all.dtype)
+            v_all[unseen] = jnp.zeros((2 * rows, v_all.shape[1]), v_all.dtype)
 
     own_codes.wait()
+    own_scales.wait()
+    scales = [scales_ref[u].astype(jnp.float32).T for u in range(slabs)]
     for b in range(width // QBLOCK):
         at = pl.ds(b * QBLOCK, QBLOCK)
         for u in range(slabs):
-            acc[u * rows:(u + 1) * rows, at] = -(codes_v[u, :, at].astype(jnp.float32)
-                                                * scales_ref[u, :, b:b + 1].astype(jnp.float32))
+            acc[u * rows:(u + 1) * rows, at] = -(codes_v[u, :, at].astype(jnp.float32) * scales[u][:, b:b + 1])
 
     for d in range(1, n_grp):
         s = jnp.maximum(g - d, 0)
@@ -270,11 +272,8 @@
             go(send(part, part, kvz_s.at[i, s], kvz_r.at[i, s], up), jnp.logical_and(here, has_up))
             go(send(part, part, kvd_s.at[i, s], kvd_r.at[i, s], other), here)
 
-    def own_up(k):
-        go(send(own_piece(k), held(g, k), up_s.at[g, k], z_r.at[g, k], up), has_up)
-
-    for k in range(SUBS // 2):
-        own_up(k)
+    for k in range(steps):
+        go(own_up(k), jnp.logical_and(mine, has_up))
 
     own_k.wait()
     own_v.wait()
@@ -319,73 +318,53 @@
 
     lax.fori_loop(0, KV_HEADS, forward, 0)
 
-    def pass_on(c, k):
-        part = placed(r, c, k)
-        arrived(part, px_s.at[0, k], px_r.at[c, k])
-        send(part, part, pd_s.at[c, k], pd_r.at[c, k], other).start()
-
-    def others(k):
-        for m in range(1, n_tp):
-            pass_on(sender(m), k)
-
-    def event(s, here, k, onward, onward_sem, to):
-        part = held(s, k)
-        pl.when(here)(functools.partial(arrived, part, up_s.at[s, k], z_r.at[s, k]))
-        go(send(part, part, onward_sem.at[s, k], z_r.at[s, k], to), jnp.logical_and(here, onward))
-        keep = jnp.logical_and(here, s == t)
-        give = jnp.logical_and(here, s != t)
-        go(send(part, placed(r, t, k), px_s.at[s, k], px_r.at[t, k], {"tp": s}), give)
-
-        @pl.when(keep)
-        def _():
-            pltpu.make_async_copy(part, placed(r, t, k), lp_s.at[k]).start()
-            send(part, placed(r, t, k), pd_s.at[t, k], pd_r.at[t, k], other).start()
-            if k > 0:
-                others(k - 1)
-
-    def from_above(d, k):
-        event(jnp.minimum(g + d, n_grp - 1), g + d < n_grp, k, has_down, down_s, down)
-
-    def from_below(d, k):
-        event(jnp.maximum(g - d, 0), g >= d, k, has_up, up_s, up)
-
-    for k in range(SUBS):
-        from_above(1, k)
-    for k in range(SUBS // 2, SUBS):
-        own_up(k)
-    for k in range(SUBS):
-        for d in range(1, n_grp):
-            from_below(d, k)
-    for d in range(2, n_grp):
-        for k in range(SUBS):
-            from_above(d, k)
-
+    rising = t < g
+    falling = t > g
+    onward_up = jnp.logical_and(rising, has_up)
+    onward_down = jnp.logical_and(falling, has_down)
+    onward = jnp.logical_or(onward_up, onward_down)
     foreign = t != g
 
-    @pl.when(foreign)
-    def _():
-        others(SUBS - 1)
-        for k in range(SUBS):
-            pltpu.make_async_copy(held(t, k), placed(r, t, k), lp_s.at[k]).wait()
-
-    pl.when(mine)(own_cols.wait)
-    for c in range(n_tp):
-        for k in range(SUBS):
-            arrived(placed(1 - r, c, k), pd_s.at[c, k], pd_r.at[c, k])
+    def relay_up(k):
+        return send(placed(r, k), placed(r, k), up_s.at[k], z_r.at[k], up)
+
+    def relay_down(k):
+        return send(placed(r, k), placed(r, k), down_s.at[k], z_r.at[k], down)
+
+    def relay_over(k):
+        return send(placed(r, k), placed(r, k), pd_s.at[k], pd_r.at[k], other)
 
     def proj_rows(kh):
         return pl.ds(pl.multiple_of(kh * feats, feats), feats)
 
-    def project(kh, carry):
+    def receive(kh):
+        for i in range(SUBS):
+            k = kh * SUBS + i
+            arrived(placed(r, k), up_s.at[k], z_r.at[k])
+            pl.when(onward_up)(lambda k=k: relay_up(k).start())
+            pl.when(onward_down)(lambda k=k: relay_down(k).start())
+            relay_over(k).start()
+
+    def project(kh):
         for m in range(1, n_tp):
             arrived(gathered.at[sender(m), kh], ag_s.at[m - 1, kh], ag_r.at[m - 1, kh])
+        for i in range(SUBS):
+            k = kh * SUBS + i
+            arrived(placed(1 - r, k), pd_s.at[k], pd_r.at[k])
         left = jnp.concatenate([gathered[u, kh] for u in range(slabs)], axis=0)
         for b in range(2):
             acc[:, b * half:(b + 1) * half] += jnp.dot(left, pq[b, proj_rows(kh)],
                                                        preferred_element_type=jnp.float32)
+
+    pl.when(mine)(own_cols.wait)
+    behind = jnp.where(onward, KV_HEADS, 0)
+
+    def collect(i, carry):
+        pl.when(jnp.logical_and(foreign, i < KV_HEADS))(lambda: receive(i))
+        pl.when(i >= behind)(lambda: project(i - behind))
         return carry
 
-    lax.fori_loop(0, KV_HEADS, project, 0)
+    lax.fori_loop(0, KV_HEADS + behind, collect, 0)
     errs[...] = acc[...].astype(jnp.bfloat16)
 
     def rs_copy(kh, m):
@@ -433,39 +412,42 @@
         gd_copy(kh).start()
 
     def gz_copy(kh, s):
-        return send(below.at[kh, s], above.at[kh, s], gz_s.at[kh, s], gz_r.at[kh, s], down)
-
-    def reduce(kh):
+        return send(below.at[kh, s], above.at[kh, g], gz_s.at[kh, s], gz_r.at[kh, g], {"grp": s})
+
+    def both_cores(kh, s):
+        return pieces[kh, r, s].astype(jnp.float32) + peer_pieces[kh, s].astype(jnp.float32)
+
+    def hand_down(kh):
         arrived(peer_pieces.at[kh], gd_s.at[kh], gd_r.at[kh])
-        for s in range(n_grp):
-            @pl.when(s <= g)
+        for s in range(n_grp - 1):
+            @pl.when(s < g)
             def _():
-                total = pieces[kh, r, s].astype(jnp.float32) + peer_pieces[kh, s].astype(jnp.float32)
-                wide_sum[...] = total
-
-                @pl.when(has_up)
-                def _():
-                    arrived(above.at[kh, s], gz_s.at[kh, s], gz_r.at[kh, s])
-                    wide_sum[...] += above[kh, s].astype(jnp.float32)
-
-                @pl.when(s < g)
-                def _():
-                    below[kh, s] = wide_sum[...].astype(jnp.bfloat16)
-                    gz_copy(kh, s).start()
-
-                @pl.when(s == g)
-                def _():
-                    done = wide_sum[...]
-                    dk_ref[0, :, kv_cols(kh)] = done[:head_dim].T.astype(jnp.bfloat16)
-                    dv_ref[0, :, kv_cols(kh)] = done[head_dim:].T.astype(jnp.bfloat16)
+                below[kh, s] = both_cores(kh, s).astype(jnp.bfloat16)
+                gz_copy(kh, s).start()
+
+    def settle(kh):
+        wide_sum[...] = both_cores(kh, g)
+        for s in range(1, n_grp):
+            @pl.when(s > g)
+            def _():
+                arrived(above.at[kh, s], gz_s.at[kh, s], gz_r.at[kh, s])
+                wide_sum[...] += above[kh, s].astype(jnp.float32)
+        done = wide_sum[...]
+        dk_ref[0, :, kv_cols(kh)] = done[:head_dim].T.astype(jnp.bfloat16)
+        dv_ref[0, :, kv_cols(kh)] = done[head_dim:].T.astype(jnp.bfloat16)
 
     def last(kh, carry):
-        pl.when(kh < KV_HEADS)(lambda: backward(kh))
-        pl.when(kh > 0)(lambda: reduce(kh - 1))
+        backward(kh)
+        hand_down(kh)
         return carry
 
+    def finish(kh, carry):
+        settle(kh)
+        return carry
+
     wide_sum = acc.at[pl.ds(0, 2 * head_dim), pl.ds(0, rows)]
-    lax.fori_loop(0, KV_HEADS + 1, last, 0)
+    lax.fori_loop(0, KV_HEADS, last, 0)
+    lax.fori_loop(0, KV_HEADS, finish, 0)
 
     for copy, when in ended:
         if when is None:
@@ -473,23 +455,33 @@
         else:
             pl.when(when)(copy.wait_send)
 
-    @pl.when(foreign)
-    def _():
-        for c in range(n_tp):
-            for k in range(SUBS):
-                part = placed(r, c, k)
-                send(part, part, pd_s.at[c, k], pd_r.at[c, k], other).wait_send()
+    def relayed(k, carry):
+        relay_over(k).wait_send()
+        pl.when(onward_up)(lambda: relay_up(k).wait_send())
+        pl.when(onward_down)(lambda: relay_down(k).wait_send())
+        return carry
+
+    pl.when(foreign)(lambda: lax.fori_loop(0, steps, relayed, None))
 
     def sent(kh, carry):
         for m in range(1, n_tp):
             ag_copy(kh, m).wait_send()
             rs_copy(kh, m).wait_send()
         gd_copy(kh).wait_send()
-        for s in range(n_grp):
+        for s in range(n_grp - 1):
             pl.when(s < g)(lambda s=s: gz_copy(kh, s).wait_send())
         return carry
 
     lax.fori_loop(0, KV_HEADS, sent, 0)
+
+
+def hand_out(dq_in, dk_in, dv_in, dq_out, dk_out, dv_out, sems):
+    pairs = ((dq_in, dq_out), (dk_in, dk_out), (dv_in, dv_out))
+    copies = [pltpu.make_async_copy(src, dst, sems.at[i]) for i, (src, dst) in enumerate(pairs)]
+    for copy in copies:
+        copy.start()
+    for copy in copies:
+        copy.wait()
 
 
 def fused(mesh, query_rows, key_rows, value_rows, teacher_codes, teacher_scales, projection):
@@ -501,44 +493,53 @@
     length = n_grp * 2 * rows
     per = HEADS // KV_HEADS
     feats = per * HEAD_DIM
-    piece = depth // n_tp
+    steps = KV_HEADS * SUBS
     low, wide = jnp.bfloat16, jnp.float32
     vmem = pltpu.VMEM
     dma = pltpu.SemaphoreType.DMA
-    hbm_spec = pl.BlockSpec(memory_space=pl.ANY)
+    hbm_spec = pl.BlockSpec(memory_space=pltpu.HBM)
+    flat_scales = teacher_scales.transpose(0, 2, 1)
     vmem_spec = pl.BlockSpec(memory_space=pltpu.VMEM)
     scratch = [
         vmem((rows, depth), low), vmem((length, kv_width), low), vmem((length, kv_width), low),
-        vmem((slabs, rows, width), low), vmem((n_grp, piece, half), low), vmem((2, depth, half), low),
+        vmem((slabs, rows, width), low), vmem(flat_scales.shape, low), vmem((2, depth, half), low),
         vmem((KV_HEADS, per * rows, length), low), vmem((KV_HEADS, per * rows, HEAD_DIM), wide),
         vmem((slabs, KV_HEADS, rows, feats), low), vmem((slabs * rows, width), wide),
         vmem((slabs * rows, width), low), vmem((KV_HEADS, slabs, rows, feats), low),
         vmem((KV_HEADS, n_tp - 1, rows, feats), low), vmem((KV_HEADS, 2, n_grp, 2 * HEAD_DIM, rows), low),
         vmem((KV_HEADS, n_grp, 2 * HEAD_DIM, rows), low), vmem((KV_HEADS, n_grp, 2 * HEAD_DIM, rows), low),
         vmem((KV_HEADS, n_grp, 2 * HEAD_DIM, rows), low),
-        dma((5,)), dma((2, n_grp)), dma((2, n_grp)), dma((2, n_grp)), dma((2, n_grp)),
-        dma((n_grp, SUBS)), dma((n_grp, SUBS)), dma((n_grp, SUBS)),
-        dma((n_grp, SUBS)), dma((n_tp, SUBS)), dma((n_tp, SUBS)), dma((n_tp, SUBS)), dma((SUBS,)),
+        dma((6,)), dma((2, n_grp)), dma((2, n_grp)), dma((2, n_grp)), dma((2, n_grp)),
+        dma((steps,)), dma((steps,)), dma((steps,)), dma((steps,)), dma((steps,)),
         dma((n_tp - 1, KV_HEADS)), dma((n_tp - 1, KV_HEADS)), dma((n_tp - 1, KV_HEADS)),
         dma((n_tp - 1, KV_HEADS)), dma((KV_HEADS,)), dma((KV_HEADS,)),
         dma((KV_HEADS, n_grp)), dma((KV_HEADS, n_grp)),
     ]
-    return pl.pallas_call(
+    outs = [jax.ShapeDtypeStruct(a.shape, a.dtype) for a in (query_rows, key_rows, value_rows)]
+    grads = pl.pallas_call(
         functools.partial(fused_kernel, n_grp, n_tp),
-        out_shape=[jax.ShapeDtypeStruct(a.shape, a.dtype) for a in (query_rows, key_rows, value_rows)],
-        in_specs=[hbm_spec] * 4 + [vmem_spec, hbm_spec],
+        out_shape=outs,
+        in_specs=[hbm_spec] * 6,
         out_specs=[vmem_spec] * 3,
         scratch_shapes=scratch,
         compiler_params=pltpu.CompilerParams(collective_id=1, has_side_effects=True,
                                              vmem_limit_bytes=60 * 2 ** 20),
-    )(query_rows, key_rows, value_rows, teacher_codes, teacher_scales, projection)
+    )(query_rows, key_rows, value_rows, teacher_codes, flat_scales, projection)
+    return pl.pallas_call(
+        hand_out,
+        out_shape=outs,
+        in_specs=[pl.BlockSpec(memory_space=pl.ANY)] * 3,
+        out_specs=[hbm_spec] * 3,
+        scratch_shapes=[dma((len(outs),))],
+        compiler_params=pltpu.CompilerParams(vmem_limit_bytes=2 ** 20),
+    )(*grads)
 
 
 def suits(mesh, teacher_codes, projection):
     depth, half = projection.shape
     n_grp, n_tp, n_rep = (mesh.shape[axis] for axis in ("grp", "tp", "rep"))
     return (n_rep == 2 and 1 < n_grp == n_tp <= NEAR and teacher_codes.shape[2] == 2 * half
-            and depth % (n_tp * SUBS * 16) == 0)
+            and depth % (KV_HEADS * SUBS * 16) == 0)
 
 
 def shards(mesh, query_rows, key_rows, value_rows, teacher_codes, teacher_scales, projection):

time: 156 us -> 115 us (0.74)
  Pallas kernels: 149 us -> 111 us
  local copies, waits for them, and re-layouts: 6.51 us -> 2.84 us
    pallas_call x1 -> x2, Pallas kernels: 149 us -> 111 us  [the longest x1 110 us: fused(): pl.pallas_call(functools.partial(fused_kernel, n_grp, n_tp), out_shape=ou...]
    unnamed x4 -> x6, local copies, waits for them, and re-layouts: 6.51 us -> 2.84 us
where the time goes in v2:
time: 115 us; the launch traced here: 114 us
  Pallas kernels  111 us (97%)
  local copies, waits for them, and re-layouts  2.84 us (2%)
    pallas_call x1, Pallas kernels, fused(): pl.pallas_call(functools.partial(fused_kernel, n_grp, n_tp), out_shape=ou...  110 us
    unnamed x6, local copies, waits for them, and re-layouts  2.84 us

profile of v2, /device:TPU:0, one launch (start us, length us, event | category | flops | bytes accessed | tf_op | source)
XLA Modules:
  0.0 114.4 jit_solution(6101785576229628863)
XLA Ops:
  0.6 110.1 %shard_map.85 = (bf16[1,128,2048]{2,1,0:T(8,128)(2,1)}, bf16[1,128,512]{2,1,0:T(8,128)(2,1)}, bf16[1,128,512]{2,1,0:T(8,128)(2,1)}) custom-call(bf16[1,128,2048]{2,1,0:T(8,128)(2,1)} %q_in.1, bf16[1,128,512]{2,1,0:T(8,128)(2,1)} %k_in.1, bf16[1,128,512]{2,1,0:T(8,128)(2,1)} %v_in.1, bf16[4,128,1024]{2,1,0:T(8,128)(2,1)} %codes_in.1, ...), custom_call_target="tpu_custom_call" | custom-call | tf_op jit(solution)/shard_map/pallas_call | solution.py:519
  110.7 0.0 copy-start
  110.7 1.0 copy-done
  111.7 0.0 copy-start.1
  111.7 0.9 copy-done.1
  112.6 0.0 copy-start.2
  112.7 0.9 copy-done.2
  113.6 0.9 shard_map.86
Async XLA Ops:
  110.7 1.0 copy-start
  111.7 0.9 copy-start.1
  112.6 0.9 copy-start.2

commit v3 on v2

--- a/solution.py
+++ b/solution.py
@@ -300,7 +300,34 @@
         part = gathered.at[t, kh]
         return send(part, part, ag_s.at[m - 1, kh], ag_r.at[m - 1, kh], peer_tp(m))
 
+    rising = t < g
+    falling = t > g
+    onward_up = jnp.logical_and(rising, has_up)
+    onward_down = jnp.logical_and(falling, has_down)
+    onward = jnp.logical_or(onward_up, onward_down)
+    foreign = t != g
+
+    def relay_up(k):
+        return send(placed(r, k), placed(r, k), up_s.at[k], z_r.at[k], up)
+
+    def relay_down(k):
+        return send(placed(r, k), placed(r, k), down_s.at[k], z_r.at[k], down)
+
+    def relay_over(k):
+        return send(placed(r, k), placed(r, k), pd_s.at[k], pd_r.at[k], other)
+
+    def receive_one(k):
+        arrived(placed(r, k), up_s.at[k], z_r.at[k])
+        pl.when(onward_up)(lambda: relay_up(k).start())
+        pl.when(onward_down)(lambda: relay_down(k).start())
+        relay_over(k).start()
+
+    def receive(kh):
+        for i in range(SUBS):
+            receive_one(kh * SUBS + i)
+
     def forward(kh, carry):
+        pl.when(onward)(lambda: receive_one(kh))
         scores = lax.dot_general(stacked_queries(kh), k_all[:, kv_cols(kh)], (((1,), (1,)), ((), ())),
                                  preferred_element_type=jnp.float32) * inv_root
         scores = jnp.where(allowed, scores, masked_low)
@@ -318,32 +345,8 @@
 
     lax.fori_loop(0, KV_HEADS, forward, 0)
 
-    rising = t < g
-    falling = t > g
-    onward_up = jnp.logical_and(rising, has_up)
-    onward_down = jnp.logical_and(falling, has_down)
-    onward = jnp.logical_or(onward_up, onward_down)
-    foreign = t != g
-
-    def relay_up(k):
-        return send(placed(r, k), placed(r, k), up_s.at[k], z_r.at[k], up)
-
-    def relay_down(k):
-        return send(placed(r, k), placed(r, k), down_s.at[k], z_r.at[k], down)
-
-    def relay_over(k):
-        return send(placed(r, k), placed(r, k), pd_s.at[k], pd_r.at[k], other)
-
     def proj_rows(kh):
         return pl.ds(pl.multiple_of(kh * feats, feats), feats)
-
-    def receive(kh):
-        for i in range(SUBS):
-            k = kh * SUBS + i
-            arrived(placed(r, k), up_s.at[k], z_r.at[k])
-            pl.when(onward_up)(lambda k=k: relay_up(k).start())
-            pl.when(onward_down)(lambda k=k: relay_down(k).start())
-            relay_over(k).start()
 
     def project(kh):
         for m in range(1, n_tp):
@@ -360,7 +363,7 @@
     behind = jnp.where(onward, KV_HEADS, 0)
 
     def collect(i, carry):
-        pl.when(jnp.logical_and(foreign, i < KV_HEADS))(lambda: receive(i))
+        pl.when(jnp.logical_and(jnp.logical_and(foreign, i < KV_HEADS), jnp.logical_or(i > 0, jnp.logical_not(onward))))(lambda: receive(i))
         pl.when(i >= behind)(lambda: project(i - behind))
         return carry
 

time: 115 us -> 110 us (0.957)
  Pallas kernels: 111 us -> 106 us
    pallas_call x1, Pallas kernels: 110 us -> 105 us  [fused(): pl.pallas_call(functools.partial(fused_kernel, n_grp, n_tp), out_shape=ou...]
where the time goes in v3:
time: 110 us; the launch traced here: 109 us
  Pallas kernels  106 us (96%)
  local copies, waits for them, and re-layouts  2.84 us (3%)
    pallas_call x1, Pallas kernels, fused(): pl.pallas_call(functools.partial(fused_kernel, n_grp, n_tp), out_shape=ou...  105 us
    unnamed x6, local copies, waits for them, and re-layouts  2.84 us

profile of v3, /device:TPU:0, one launch (start us, length us, event | category | flops | bytes accessed | tf_op | source)
XLA Modules:
  0.0 109.4 jit_solution(7185421006279812541)
XLA Ops:
  0.6 105.0 %shard_map.85 = (bf16[1,128,2048]{2,1,0:T(8,128)(2,1)}, bf16[1,128,512]{2,1,0:T(8,128)(2,1)}, bf16[1,128,512]{2,1,0:T(8,128)(2,1)}) custom-call(bf16[1,128,2048]{2,1,0:T(8,128)(2,1)} %q_in.1, bf16[1,128,512]{2,1,0:T(8,128)(2,1)} %k_in.1, bf16[1,128,512]{2,1,0:T(8,128)(2,1)} %v_in.1, bf16[4,128,1024]{2,1,0:T(8,128)(2,1)} %codes_in.1, ...), custom_call_target="tpu_custom_call" | custom-call | tf_op jit(solution)/shard_map/pallas_call | solution.py:522
  105.6 0.0 copy-start
  105.6 1.0 copy-done
  106.6 0.0 copy-start.1
  106.7 0.9 copy-done.1
  107.6 0.0 copy-start.2
  107.6 0.9 copy-done.2
  108.5 0.9 shard_map.86
Async XLA Ops:
  105.6 1.0 copy-start
  106.6 0.9 copy-start.1
  107.6 0.9 copy-start.2

commit v4 on v3

--- a/solution.py
+++ b/solution.py
@@ -150,12 +150,13 @@
 
 NEAR = 4
 SUBS = 4
+SPARE = 2
 
 
 def fused_kernel(n_grp, n_tp, q_in, k_in, v_in, codes_in, scales_in, proj_in, dq_ref, dk_ref, dv_ref,
-                 q_v, k_all, v_all, codes_v, scales_ref, pq, probs, wide, gathered, acc, errs, terms, sums,
+                 q_v, k_all, v_all, codes_v, scales_ref, pq, stage, probs, wide, gathered, acc, errs, terms, sums,
                  pieces, peer_pieces, above, below, lsem, kvz_s, kvz_r, kvd_s, kvd_r, up_s, down_s, z_r,
-                 pd_s, pd_r, ag_s, ag_r, rs_s, rs_r, gd_s, gd_r, gz_s, gz_r):
+                 pd_s, pd_r, zz_s, zz_r, zx_s, ag_s, ag_r, rs_s, rs_r, gd_s, gd_r, gz_s, gz_r):
     g = lax.axis_index("grp")
     t = lax.axis_index("tp")
     r = lax.axis_index("rep")
@@ -272,8 +273,36 @@
             go(send(part, part, kvz_s.at[i, s], kvz_r.at[i, s], up), jnp.logical_and(here, has_up))
             go(send(part, part, kvd_s.at[i, s], kvd_r.at[i, s], other), here)
 
-    for k in range(steps):
+    direct = steps - SPARE
+    idle = t == n_tp - 1
+
+    def spare_up(s, a, own=False):
+        src = proj_in.at[span(direct + a)] if own else stage.at[s, a]
+        return send(src, stage.at[s, a], zz_s.at[s, a], zz_r.at[s, a], up)
+
+    def spare_out(s, a):
+        return send(stage.at[s, a], placed(r, direct + a), zx_s.at[s, a], z_r.at[direct + a], {"tp": s})
+
+    for k in range(direct):
         go(own_up(k), jnp.logical_and(mine, has_up))
+    for s in range(n_grp - 1):
+        for a in range(SPARE):
+            go(spare_up(s, a, own=True), jnp.logical_and(idle, g == s))
+
+    def spare_in(act, wait):
+        for s in range(n_grp - 2, -1, -1):
+            for a in range(SPARE):
+                @pl.when(jnp.logical_and(idle, g > s))
+                def _(s=s, a=a):
+                    if wait:
+                        arrived(stage.at[s, a], zz_s.at[s, a], zz_r.at[s, a])
+                    pl.when(has_up)(lambda: act(spare_up(s, a)))
+                    act(spare_out(s, a))
+
+    def begin(copy):
+        copy.start()
+
+    pl.when(g == 1)(lambda: spare_in(begin, True))
 
     own_k.wait()
     own_v.wait()
@@ -318,7 +347,7 @@
 
     def receive_one(k):
         arrived(placed(r, k), up_s.at[k], z_r.at[k])
-        pl.when(onward_up)(lambda: relay_up(k).start())
+        pl.when(jnp.logical_and(onward_up, k < direct))(lambda: relay_up(k).start())
         pl.when(onward_down)(lambda: relay_down(k).start())
         relay_over(k).start()
 
@@ -364,6 +393,7 @@
 
     def collect(i, carry):
         pl.when(jnp.logical_and(jnp.logical_and(foreign, i < KV_HEADS), jnp.logical_or(i > 0, jnp.logical_not(onward))))(lambda: receive(i))
+        pl.when(jnp.logical_and(g > 1, i == jnp.where(onward, 1, 0)))(lambda: spare_in(begin, True))
         pl.when(i >= behind)(lambda: project(i - behind))
         return carry
 
@@ -458,9 +488,11 @@
         else:
             pl.when(when)(copy.wait_send)
 
+    spare_in(lambda copy: copy.wait_send(), False)
+
     def relayed(k, carry):
         relay_over(k).wait_send()
-        pl.when(onward_up)(lambda: relay_up(k).wait_send())
+        pl.when(jnp.logical_and(onward_up, k < direct))(lambda: relay_up(k).wait_send())
         pl.when(onward_down)(lambda: relay_down(k).wait_send())
         return carry
 
@@ -506,6 +538,7 @@
     scratch = [
         vmem((rows, depth), low), vmem((length, kv_width), low), vmem((length, kv_width), low),
         vmem((slabs, rows, width), low), vmem(flat_scales.shape, low), vmem((2, depth, half), low),
+        vmem((n_grp - 1, SPARE, depth // steps, half), low),
         vmem((KV_HEADS, per * rows, length), low), vmem((KV_HEADS, per * rows, HEAD_DIM), wide),
         vmem((slabs, KV_HEADS, rows, feats), low), vmem((slabs * rows, width), wide),
         vmem((slabs * rows, width), low), vmem((KV_HEADS, slabs, rows, feats), low),
@@ -514,6 +547,7 @@
         vmem((KV_HEADS, n_grp, 2 * HEAD_DIM, rows), low),
         dma((6,)), dma((2, n_grp)), dma((2, n_grp)), dma((2, n_grp)), dma((2, n_grp)),
         dma((steps,)), dma((steps,)), dma((steps,)), dma((steps,)), dma((steps,)),
+        dma((n_grp - 1, SPARE)), dma((n_grp - 1, SPARE)), dma((n_grp - 1, SPARE)),
         dma((n_tp - 1, KV_HEADS)), dma((n_tp - 1, KV_HEADS)), dma((n_tp - 1, KV_HEADS)),
         dma((n_tp - 1, KV_HEADS)), dma((KV_HEADS,)), dma((KV_HEADS,)),
         dma((KV_HEADS, n_grp)), dma((KV_HEADS, n_grp)),

time: 110 us -> 109 us (level)
  Pallas kernels: 106 us -> 104 us
    pallas_call x1, Pallas kernels: 105 us -> 103 us  [fused(): pl.pallas_call(functools.partial(fused_kernel, n_grp, n_tp), out_shape=ou...]
where the time goes in v4:
time: 109 us; the launch traced here: 107 us
  Pallas kernels  104 us (95%)
  local copies, waits for them, and re-layouts  2.84 us (3%)
    pallas_call x1, Pallas kernels, fused(): pl.pallas_call(functools.partial(fused_kernel, n_grp, n_tp), out_shape=ou...  103 us
    unnamed x6, local copies, waits for them, and re-layouts  2.84 us

profile of v4, /device:TPU:0, one launch (start us, length us, event | category | flops | bytes accessed | tf_op | source)
XLA Modules:
  0.0 107.5 jit_solution(12128741364730585934)
XLA Ops:
  0.6 103.1 %shard_map.85 = (bf16[1,128,2048]{2,1,0:T(8,128)(2,1)}, bf16[1,128,512]{2,1,0:T(8,128)(2,1)}, bf16[1,128,512]{2,1,0:T(8,128)(2,1)}) custom-call(bf16[1,128,2048]{2,1,0:T(8,128)(2,1)} %q_in.1, bf16[1,128,512]{2,1,0:T(8,128)(2,1)} %k_in.1, bf16[1,128,512]{2,1,0:T(8,128)(2,1)} %v_in.1, bf16[4,128,1024]{2,1,0:T(8,128)(2,1)} %codes_in.1, ...), custom_call_target="tpu_custom_call" | custom-call | tf_op jit(solution)/shard_map/pallas_call | solution.py:556
  103.7 0.0 copy-start
  103.7 1.0 copy-done
  104.8 0.0 copy-start.1
  104.8 0.9 copy-done.1
  105.7 0.0 copy-start.2
  105.7 0.9 copy-done.2
  106.6 0.9 shard_map.86
Async XLA Ops:
  103.7 1.0 copy-start
  104.8 0.9 copy-start.1
  105.7 0.9 copy-start.2
